TPU v7x, 32 devices: a whole 2x2x4 slice. The times are simulated.
32 devices in a mesh: groups: 2 (over x), rows: 16 (over z, y, core).
Axes of the slice: x: 2, y: 2, z: 4, core: 2. Of those that a mesh axis runs over, the one named last changes fastest.
Arguments:
- tap_two: bfloat16 [6144, 1024], P(('groups', 'rows')), parts along dimension 0, may hold values from -6 to 6
- coarse_path: bfloat16 [6144, 256], P(('groups', 'rows')), parts along dimension 0, may hold values from -6 to 6
- proj_weight: bfloat16 [1024, 512], replicated, may hold values from -0.1875 to 0.1875
- proj_bias: float32 [512], replicated, may hold values from -3 to 3
- lift_weight: bfloat16 [512, 2048], replicated, may hold values from -0.25 to 0.25
- lift_bias: float32 [512], replicated, may hold values from -3 to 3
- merge_weight: bfloat16 [4608, 256], replicated, may hold values from -0.09375 to 0.09375
- out_weight: bfloat16 [256, 256], replicated, may hold values from -0.375 to 0.375
- out_bias: float32 [256], replicated, may hold values from -3 to 3
- first_inner_w: bfloat16 [2304, 256], replicated, may hold values from -0.125 to 0.125
- first_inner_b: float32 [256], replicated, may hold values from -3 to 3
- first_outer_w: bfloat16 [2304, 256], replicated, may hold values from -0.125 to 0.125
- first_outer_b: float32 [256], replicated, may hold values from -3 to 3
- second_inner_w: bfloat16 [2304, 256], replicated, may hold values from -0.125 to 0.125
- second_inner_b: float32 [256], replicated, may hold values from -3 to 3
- second_outer_w: bfloat16 [2304, 256], replicated, may hold values from -0.125 to 0.125
- second_outer_b: float32 [256], replicated, may hold values from -3 to 3
Outputs:
- united: bfloat16 [64, 384, 256], P(('groups', 'rows')), parts along dimension 0
There are 2 independent parts, one for each index of `groups`. A program takes and returns all parts, laid end to end along the dimension named above; an argument that names none is the same for every part. Nothing has to cross between parts.
All inputs are finite; a program needn't handle non-finite values.
Results may differ from a plain program's by a relative error of at most 0.0075.
Values may be sent and summed in bfloat16 or wider, within the bound.
A program may use at most 64 MiB of HBM per device.

v0:
```python
import functools

import jax
import jax.numpy as jnp
from jax import lax
from jax.experimental import pallas as pl
from jax.experimental.pallas import tpu as pltpu
from jax.sharding import PartitionSpec as P

GW = 192
BF16 = jnp.bfloat16
F32 = jnp.float32

PJ_SIB, PJ_ONE, PJ_TWO, PJ_THREE, CO_SIB, CO_ONE, CO_TWO, S_REA, S_IN1, S_MER, S_IN2 = range(11)


def dot(a, b):
    return jnp.dot(a, b, preferred_element_type=F32)


def put(slab, row, even, odd):
    width, chans = even.shape
    at = lax.broadcasted_iota(jnp.int32, even.shape, 0)
    before = jnp.where(at == 0, 0.0, pltpu.roll(odd, 1, 0))
    after = jnp.where(at == width - 1, 0.0, pltpu.roll(even, width - 1, 0))
    for group, value in enumerate((before, even, odd, after)):
        slab[row, :, group * chans : (group + 1) * chans] = value.astype(BF16)


def kernel(
    count,
    tap_h,
    coarse_h,
    proj_h,
    proj_bh,
    lift_h,
    lift_bh,
    merge_h,
    out_h,
    out_bh,
    fi_h,
    fi_bh,
    fo_h,
    fo_bh,
    si_h,
    si_bh,
    so_h,
    so_bh,
    result,
    tap,
    coarse,
    proj_w,
    proj_b,
    lift_w,
    lift_b,
    merge_w,
    out_w,
    out_b,
    fi_w,
    fi_b,
    fo_w,
    fo_b,
    si_w,
    si_b,
    so_w,
    so_b,
    pj,
    wid,
    rea,
    rea_raw,
    carried,
    in1,
    mer,
    mer_raw,
    in2,
    local_sem,
    send_sem,
    recv_sem,
):
    width = tap.shape[0]
    feat = proj_w.shape[1]
    chans = out_w.shape[1]
    me = lax.axis_index("rows")
    side = lax.rem(me, 2)
    step = 2 * side - 1
    sibling = me - step

    def inside(device):
        return jnp.logical_and(device >= 0, device < count)

    valid = (True, inside(me + step), inside(me + 2 * step), inside(me + 3 * step))
    back_two = inside(me - 2 * step)

    started = []

    def fetch(src, dst):
        copy = pltpu.make_async_copy(src, dst, local_sem.at[len(started)])
        started.append(copy)
        copy.start()
        return [copy]

    def fetch_conv(src, dst):
        part = src.shape[0] // 3
        copies = []
        for k in range(3):
            where = pl.multiple_of((side * k + (1 - side) * (2 - k)) * part, part)
            copies += fetch(src.at[pl.ds(where, part)], dst.at[pl.ds(k * part, part)])
        return copies

    def done(copies):
        for copy in copies:
            copy.wait()

    coarse_in = fetch(coarse_h, coarse.at[0])
    tap_in = fetch(tap_h, tap) + fetch(proj_h, proj_w) + fetch(proj_bh, proj_b)
    lift_in = fetch(lift_bh, lift_b)
    half = 2 * feat
    for m in range(2):
        where = pl.multiple_of((side * m + (1 - side) * (1 - m)) * half, half)
        lift_in += fetch(lift_h.at[:, pl.ds(where, half)], lift_w.at[:, pl.ds(m * half, half)])

    partners = (
        (me + step, valid[1]),
        (me + 2 * step, valid[2]),
        (me - 2 * step, back_two),
        (me + 3 * step, valid[3]),
    )
    barrier = pltpu.get_barrier_semaphore()
    expected = jnp.int32(1)
    pl.semaphore_signal(
        barrier, inc=1, device_id={"rows": sibling}, device_id_type=pl.DeviceIdType.MESH
    )
    for device, there in partners:

        @pl.when(there)
        def _():
            pl.semaphore_signal(
                barrier, inc=1, device_id={"rows": device}, device_id_type=pl.DeviceIdType.MESH
            )

        expected = expected + there.astype(jnp.int32)
    pl.semaphore_wait(barrier, expected)

    def remote(src, dst, kind, device):
        return pltpu.make_async_remote_copy(
            src_ref=src,
            dst_ref=dst,
            send_sem=send_sem.at[kind],
            recv_sem=recv_sem.at[kind],
            device_id={"rows": device},
            device_id_type=pl.DeviceIdType.MESH,
        )

    sent = []

    def send(src, dst, kind, device, there=None):
        sent.append((remote(src, dst, kind, device), there))
        if there is None:
            sent[-1][0].start()
        else:
            pl.when(there)(sent[-1][0].start)

    def received(dst, kind, there=None):
        copy = remote(dst, dst, kind, sibling)
        if there is None:
            copy.wait_recv()
        else:
            pl.when(there)(copy.wait_recv)

    done(coarse_in)
    send(coarse.at[0], coarse.at[3], CO_SIB, sibling)

    merge_in = fetch_conv(merge_h, merge_w)
    out_in = fetch(out_h, out_w) + fetch(out_bh, out_b)
    fi_in = fetch(fi_bh, fi_b) + fetch_conv(fi_h, fi_w)
    fo_in = fetch(fo_bh, fo_b) + fetch_conv(fo_h, fo_w)
    si_in = fetch(si_bh, si_b) + fetch_conv(si_h, si_w)
    so_in = fetch(so_bh, so_b) + fetch_conv(so_h, so_w)

    done(tap_in)
    pj[0] = (dot(tap[...], proj_w[...]) + proj_b[...]).astype(BF16)
    send(pj.at[0], pj.at[1], PJ_ONE, me + step, valid[1])
    send(pj.at[0], pj.at[4], PJ_SIB, sibling)
    send(pj.at[0], pj.at[3], PJ_THREE, me + 3 * step, valid[3])
    send(coarse.at[0], coarse.at[1], CO_ONE, me + step, valid[1])
    at_end = jnp.logical_and(back_two, jnp.logical_not(valid[1]))
    send(pj.at[0], pj.at[2], PJ_TWO, me - 2 * step, at_end)
    send(coarse.at[0], coarse.at[2], CO_TWO, me - 2 * step, at_end)

    def lift(token, slab_token, halves):
        for m in halves:
            both = dot(pj[slab_token], lift_w[:, m * half : (m + 1) * half])
            even = both[:, :feat] + lift_b[...]
            odd = both[:, feat:] + lift_b[...]
            if token > 0:
                even = jnp.where(valid[token], even, 0.0)
                odd = jnp.where(valid[token], odd, 0.0)
            put(wid, 2 * token + m + 1, even, odd)

    def conv(slab, weight, low, high):
        group = slab.shape[2] // 4
        rows = high - low
        sides = []
        for parity in range(2):
            total = None
            for k in range(3):
                cells = slab[low + k : high + k, :, parity * group : (parity + 3) * group]
                term = dot(
                    cells.reshape(rows * width, 3 * group),
                    weight[k * 3 * group : (k + 1) * 3 * group, :],
                )
                total = term if total is None else total + term
            sides.append(total.reshape(rows, width, chans))
        return sides

    def keep(row, value):
        return value if row < 2 else jnp.where(valid[row // 2], value, 0.0)

    def merge_rows(low, high):
        even, odd = conv(wid, merge_w, low, high)
        for row in range(low, high):
            e, o = keep(row, even[row - low]), keep(row, odd[row - low])
            if row < 4:
                rea_raw[row, :, :chans] = e.astype(BF16)
                rea_raw[row, :, chans:] = o.astype(BF16)
            put(rea, row + 1, jnp.maximum(e, 0.0), jnp.maximum(o, 0.0))

    def inner_rows(src, weight, bias, dst, low, high):
        even, odd = conv(src, weight, low, high)
        for row in range(low, high):
            e = jnp.maximum(even[row - low] + bias[...], 0.0)
            o = jnp.maximum(odd[row - low] + bias[...], 0.0)
            put(dst, row + 1, keep(row, e), keep(row, o))

    def merged_rows(low, high):
        even, odd = conv(in1, fo_w, low, high)
        for row in range(low, high):
            outer = []
            for parity, value in enumerate((even, odd)):
                lanes = slice(parity * chans, (parity + 1) * chans)
                whole = (
                    value[row - low]
                    + fo_b[...]
                    + rea_raw[row, :, lanes].astype(F32)
                    + carried[row, :, lanes]
                )
                whole = keep(row, whole)
                if row < 2:
                    mer_raw[row, :, lanes] = whole.astype(BF16)
                outer.append(jnp.maximum(whole, 0.0))
            put(mer, row + 1, *outer)

    def carry(row, near, far):
        band = 0.75 * coarse[near].astype(F32) + 0.25 * coarse[far].astype(F32)
        at = lax.broadcasted_iota(jnp.int32, band.shape, 0)
        before = jnp.where(at == 0, band, pltpu.roll(band, 1, 0))
        after = jnp.where(at == width - 1, band, pltpu.roll(band, width - 1, 0))
        for parity, other in enumerate((before, after)):
            spread = (0.75 * band + 0.25 * other).astype(BF16)
            carried[row, :, parity * chans : (parity + 1) * chans] = (
                dot(spread, out_w[...]) + out_b[...]
            )

    done(lift_in)
    lift(0, 0, (0, 1))
    received(pj.at[4], PJ_SIB)
    lift(-1, 4, (1,))
    done(merge_in)
    merge_rows(0, 1)
    send(rea.at[1], rea.at[0], S_REA, sibling)

    done(out_in)
    received(coarse.at[3], CO_SIB)
    carry(0, 0, 3)

    @pl.when(jnp.logical_not(valid[1]))
    def _():
        coarse[1] = coarse[0]
        pj[1] = jnp.zeros_like(pj[1])

    received(pj.at[1], PJ_ONE, valid[1])
    send(pj.at[1], pj.at[2], PJ_TWO, me + 3 * step, valid[3])
    lift(1, 1, (0, 1))
    received(coarse.at[1], CO_ONE, valid[1])
    send(coarse.at[1], coarse.at[2], CO_TWO, me + 3 * step, valid[3])
    merge_rows(1, 3)
    received(rea.at[0], S_REA)
    done(fi_in)
    inner_rows(rea, fi_w, fi_b, in1, 0, 1)
    send(in1.at[1], in1.at[0], S_IN1, sibling)
    inner_rows(rea, fi_w, fi_b, in1, 1, 2)
    done(fo_in)
    received(in1.at[0], S_IN1)
    merged_rows(0, 1)
    send(mer.at[1], mer.at[0], S_MER, sibling)

    @pl.when(jnp.logical_not(valid[2]))
    def _():
        pj[2] = jnp.zeros_like(pj[2])

    @pl.when(jnp.logical_not(valid[3]))
    def _():
        pj[3] = jnp.zeros_like(pj[3])

    carry(1, 0, 1)
    carry(2, 1, 0)
    received(pj.at[2], PJ_TWO, valid[2])
    lift(2, 2, (0, 1))
    received(pj.at[3], PJ_THREE, valid[3])
    lift(3, 3, (0,))
    merge_rows(3, 6)
    inner_rows(rea, fi_w, fi_b, in1, 2, 5)

    @pl.when(jnp.logical_not(valid[2]))
    def _():
        coarse[2] = coarse[1]

    received(coarse.at[2], CO_TWO, valid[2])
    carry(3, 1, 2)
    merged_rows(1, 4)
    done(si_in)
    received(mer.at[0], S_MER)
    inner_rows(mer, si_w, si_b, in2, 0, 1)
    send(in2.at[1], in2.at[0], S_IN2, sibling)
    inner_rows(mer, si_w, si_b, in2, 1, 3)
    done(so_in)

    line = lax.broadcasted_iota(jnp.int32, (2 * width, 2 * width), 0)
    column = lax.broadcasted_iota(jnp.int32, (2 * width, 2 * width), 1)
    weave = (column == line // 2 + width * (line % 2)).astype(F32).astype(BF16)
    for row in (1, 0):
        if row == 0:
            received(in2.at[0], S_IN2)
        sides = conv(in2, so_w, row, row + 1)
        united = [
            (sides[parity][0] + so_b[...] + mer_raw[row, :, parity * chans : (parity + 1) * chans].astype(F32)).astype(BF16)
            for parity in range(2)
        ]
        woven = dot(weave, jnp.concatenate(united, axis=0)).astype(BF16)
        target = side * row + (1 - side) * (1 - row)
        result[pl.ds(target, 1)] = woven[None]

    for copy, there in sent:
        if there is None:
            copy.wait_send()
        else:
            pl.when(there)(copy.wait_send)


def body(*args):
    count = lax.axis_size("rows")
    tap_two, coarse_path, proj_weight = args[:3]
    tokens, depth = tap_two.shape
    feat, chans = proj_weight.shape[1], coarse_path.shape[1]
    assert tokens == GW and count % 2 == 0
    args = [arg.reshape(1, -1) if arg.ndim == 1 else arg for arg in args]

    scratch = []
    for place, arg in enumerate(args):
        shape = (4, *arg.shape) if place == 1 else arg.shape
        scratch.append(pltpu.VMEM(shape, arg.dtype))
    scratch += [
        pltpu.VMEM((5, tokens, feat), BF16),
        pltpu.VMEM((8, tokens, 4 * feat), BF16),
        pltpu.VMEM((7, tokens, 4 * chans), BF16),
        pltpu.VMEM((4, tokens, 2 * chans), BF16),
        pltpu.VMEM((4, tokens, 2 * chans), F32),
        pltpu.VMEM((6, tokens, 4 * chans), BF16),
        pltpu.VMEM((5, tokens, 4 * chans), BF16),
        pltpu.VMEM((2, tokens, 2 * chans), BF16),
        pltpu.VMEM((4, tokens, 4 * chans), BF16),
        pltpu.SemaphoreType.DMA((28,)),
        pltpu.SemaphoreType.DMA((11,)),
        pltpu.SemaphoreType.DMA((11,)),
    ]
    return pl.pallas_call(
        functools.partial(kernel, count),
        out_shape=jax.ShapeDtypeStruct((2, 2 * tokens, chans), BF16),
        in_specs=[pl.BlockSpec(memory_space=pl.ANY)] * len(args),
        out_specs=pl.BlockSpec(memory_space=pltpu.VMEM),
        scratch_shapes=scratch,
        compiler_params=pltpu.CompilerParams(
            collective_id=0, has_side_effects=True, vmem_limit_bytes=60 * 2**20
        ),
        name="fused_tap",
    )(*args)


def solution(mesh):
    return jax.shard_map(
        body,
        mesh=mesh,
        in_specs=(P(("groups", "rows"), None),) * 2 + (P(),) * 15,
        out_specs=P(("groups", "rows"), None, None),
        check_vma=False,
    )
```

profile of v0, /device:TPU:27, one launch (start us, length us, event | category | flops | bytes accessed | tf_op | source)
XLA Modules:
  0.0 31.9 jit_solution(5939754371829068932)
XLA Ops:
  0.0 30.2 %fused_tap.1 = bf16[2,384,256]{2,1,0:T(8,128)(2,1)} custom-call(bf16[192,1024]{1,0:T(8,128)(2,1)} %tap_h.1, bf16[192,256]{1,0:T(8,128)(2,1)} %coarse_h.1, bf16[1024,512]{1,0:T(8,128)(2,1)} %proj_h.1, f32[1,512]{1,0:T(1,128)} %bitcast.7, bf16[512,2048]{1,0:T(8,128)(2,1)} %lift_h.1, f32[1,512]{1,0:T(1,128)} %bitcast.8, bf16[4608,256]{1,0:T(8,128)(2,1)} %merge_h.1, ...), custom_call_target="tpu_custom_call" | custom-call | tf_op jit(solution)/shard_map/fused_tap/pallas_call | solution.py:376
  30.2 1.8 %copy.19 = bf16[2,384,256]{2,1,0:T(8,128)(2,1)} copy(bf16[2,384,256]{2,1,0:T(8,128)(2,1)} %fused_tap.1) | data formatting | bytes 786432
where the time goes:
time: 32.3 us; the launch traced here: 31.9 us
  Pallas kernels  30.2 us (93%)
  local copies, waits for them, and re-layouts  1.77 us (5%)
    pallas_call x1, Pallas kernels, body(): pl.pallas_call(functools.partial(kernel, count), out_shape=jax.ShapeDtype...  30.2 us
    unnamed x1, local copies, waits for them, and re-layouts  1.77 us

commit v1 on v0

--- a/solution.py
+++ b/solution.py
@@ -373,9 +373,9 @@
         pltpu.SemaphoreType.DMA((11,)),
         pltpu.SemaphoreType.DMA((11,)),
     ]
-    return pl.pallas_call(
+    mid = pl.pallas_call(
         functools.partial(kernel, count),
-        out_shape=jax.ShapeDtypeStruct((2, 2 * tokens, chans), BF16),
+        out_shape=pltpu.VMEM((2, 2 * tokens, chans), BF16),
         in_specs=[pl.BlockSpec(memory_space=pl.ANY)] * len(args),
         out_specs=pl.BlockSpec(memory_space=pltpu.VMEM),
         scratch_shapes=scratch,
@@ -385,6 +385,8 @@
         name="fused_tap",
     )(*args)
 
+    return mid
+
 
 def solution(mesh):
     return jax.shard_map(

time: 32.3 us -> 30.6 us (0.947)
  local copies, waits for them, and re-layouts: 1.77 us -> 0.75 us
  Pallas kernels: 30.2 us -> 29.4 us
    unnamed x1, local copies, waits for them, and re-layouts: 1.77 us -> 0.75 us
    pallas_call x1, Pallas kernels: 30.2 us -> 29.4 us  [body(): pl.pallas_call(functools.partial(kernel, count), out_shape=pltpu.VMEM((2,...]
where the time goes in v1:
time: 30.6 us; the launch traced here: 30.2 us
  Pallas kernels  29.4 us (96%)
  local copies, waits for them, and re-layouts  0.75 us (2%)
    pallas_call x1, Pallas kernels, body(): pl.pallas_call(functools.partial(kernel, count), out_shape=pltpu.VMEM((2,...  29.4 us
    unnamed x1, local copies, waits for them, and re-layouts  0.75 us

profile of v1, /device:TPU:27, one launch (start us, length us, event | category | flops | bytes accessed | tf_op | source)
XLA Modules:
  0.0 30.2 jit_solution(16803903982740990562)
XLA Ops:
  0.0 29.4 %fused_tap.1 = bf16[2,384,256]{2,1,0:T(8,128)(2,1)S(1)} custom-call(bf16[192,1024]{1,0:T(8,128)(2,1)} %tap_h.1, bf16[192,256]{1,0:T(8,128)(2,1)} %coarse_h.1, bf16[1024,512]{1,0:T(8,128)(2,1)} %proj_h.1, f32[1,512]{1,0:T(1,128)} %bitcast.7, bf16[512,2048]{1,0:T(8,128)(2,1)} %lift_h.1, f32[1,512]{1,0:T(1,128)} %bitcast.8, bf16[4608,256]{1,0:T(8,128)(2,1)} %merge_h.1, ...), custom_call_target="tpu_custom_call" | custom-call | tf_op jit(solution)/shard_map/fused_tap/pallas_call | solution.py:376
  29.4 0.7 %copy.19 = bf16[2,384,256]{2,1,0:T(8,128)(2,1)} copy(bf16[2,384,256]{2,1,0:T(8,128)(2,1)S(1)} %fused_tap.1) | data formatting | bytes 786432

commit v2 on v1

--- a/solution.py
+++ b/solution.py
@@ -11,7 +11,12 @@
 BF16 = jnp.bfloat16
 F32 = jnp.float32
 
-PJ_SIB, PJ_ONE, PJ_TWO, PJ_THREE, CO_SIB, CO_ONE, CO_TWO, S_REA, S_IN1, S_MER, S_IN2 = range(11)
+PIECES = 2
+PJ_SIB, PJ_THREE, CO_SIB, CO_ONE, CO_TWO, S_REA, S_IN1, S_MER, S_FAR = range(9)
+PJ_ONE = 9
+PJ_TWO = PJ_ONE + PIECES
+KINDS = PJ_TWO + PIECES
+STRIP = 64
 
 
 def dot(a, b):
@@ -21,10 +26,26 @@
 def put(slab, row, even, odd):
     width, chans = even.shape
     at = lax.broadcasted_iota(jnp.int32, even.shape, 0)
-    before = jnp.where(at == 0, 0.0, pltpu.roll(odd, 1, 0))
-    after = jnp.where(at == width - 1, 0.0, pltpu.roll(even, width - 1, 0))
-    for group, value in enumerate((before, even, odd, after)):
-        slab[row, :, group * chans : (group + 1) * chans] = value.astype(BF16)
+    before = jnp.where(at == 0, 0.0, pltpu.roll(odd, 1, 0)).astype(BF16)
+    after = jnp.where(at == width - 1, 0.0, pltpu.roll(even, width - 1, 0)).astype(BF16)
+    even, odd = even.astype(BF16), odd.astype(BF16)
+    for group, value in enumerate((before - odd, even + odd, even - after, odd - even)):
+        slab[row, :, group * chans : (group + 1) * chans] = value
+
+
+def prepare(weight):
+    depth = weight.shape[2]
+
+    def strip(step, carry):
+        rows = pl.ds(pl.multiple_of(step * STRIP, STRIP), STRIP)
+        for k in range(3):
+            outer = 0.5 * (weight[0, k, rows, :].astype(F32) + weight[2, k, rows, :].astype(F32))
+            inner = 0.5 * weight[1, k, rows, :].astype(F32)
+            weight[1, k, rows, :] = (outer + inner).astype(BF16)
+            weight[3, k, rows, :] = (outer - inner).astype(BF16)
+        return carry
+
+    lax.fori_loop(0, depth // STRIP, strip, 0)
 
 
 def kernel(
@@ -100,19 +121,17 @@
         return [copy]
 
     def fetch_conv(src, dst):
-        part = src.shape[0] // 3
         copies = []
         for k in range(3):
-            where = pl.multiple_of((side * k + (1 - side) * (2 - k)) * part, part)
-            copies += fetch(src.at[pl.ds(where, part)], dst.at[pl.ds(k * part, part)])
+            copies += fetch(src.at[side * k + (1 - side) * (2 - k)], dst.at[pl.ds(0, 3), k])
         return copies
 
     def done(copies):
         for copy in copies:
             copy.wait()
 
+    tap_in = fetch(tap_h, tap) + fetch(proj_h, proj_w) + fetch(proj_bh, proj_b)
     coarse_in = fetch(coarse_h, coarse.at[0])
-    tap_in = fetch(tap_h, tap) + fetch(proj_h, proj_w) + fetch(proj_bh, proj_b)
     lift_in = fetch(lift_bh, lift_b)
     half = 2 * feat
     for m in range(2):
@@ -139,7 +158,6 @@
             )
 
         expected = expected + there.astype(jnp.int32)
-    pl.semaphore_wait(barrier, expected)
 
     def remote(src, dst, kind, device):
         return pltpu.make_async_remote_copy(
@@ -167,25 +185,32 @@
         else:
             pl.when(there)(copy.wait_recv)
 
-    done(coarse_in)
-    send(coarse.at[0], coarse.at[3], CO_SIB, sibling)
-
+    done(tap_in)
     merge_in = fetch_conv(merge_h, merge_w)
     out_in = fetch(out_h, out_w) + fetch(out_bh, out_b)
     fi_in = fetch(fi_bh, fi_b) + fetch_conv(fi_h, fi_w)
     fo_in = fetch(fo_bh, fo_b) + fetch_conv(fo_h, fo_w)
     si_in = fetch(si_bh, si_b) + fetch_conv(si_h, si_w)
     so_in = fetch(so_bh, so_b) + fetch_conv(so_h, so_w)
-
-    done(tap_in)
     pj[0] = (dot(tap[...], proj_w[...]) + proj_b[...]).astype(BF16)
-    send(pj.at[0], pj.at[1], PJ_ONE, me + step, valid[1])
+
+    piece = width // PIECES
+
+    def part(slot, k):
+        return pj.at[slot, pl.ds(k * piece, piece)]
+
+    pl.semaphore_wait(barrier, expected)
+    at_end = jnp.logical_and(back_two, jnp.logical_not(valid[1]))
+    for k in range(PIECES):
+        send(part(0, k), part(1, k), PJ_ONE + k, me + step, valid[1])
+        send(part(0, k), part(2, k), PJ_TWO + k, me - 2 * step, at_end)
     send(pj.at[0], pj.at[4], PJ_SIB, sibling)
-    send(pj.at[0], pj.at[3], PJ_THREE, me + 3 * step, valid[3])
-    send(coarse.at[0], coarse.at[1], CO_ONE, me + step, valid[1])
-    at_end = jnp.logical_and(back_two, jnp.logical_not(valid[1]))
-    send(pj.at[0], pj.at[2], PJ_TWO, me - 2 * step, at_end)
-    send(coarse.at[0], coarse.at[2], CO_TWO, me - 2 * step, at_end)
+    done(coarse_in)
+    send(coarse.at[0], coarse.at[3], CO_SIB, sibling)
+
+    def pass_on(k):
+        received(part(1, k), PJ_ONE + k, valid[1])
+        send(part(1, k), part(2, k), PJ_TWO + k, me + 3 * step, valid[3])
 
     def lift(token, slab_token, halves):
         for m in halves:
@@ -197,21 +222,22 @@
                 odd = jnp.where(valid[token], odd, 0.0)
             put(wid, 2 * token + m + 1, even, odd)
 
-    def conv(slab, weight, low, high):
+    def conv(slab, weight, low, high, base=1):
         group = slab.shape[2] // 4
         rows = high - low
-        sides = []
-        for parity in range(2):
-            total = None
-            for k in range(3):
-                cells = slab[low + k : high + k, :, parity * group : (parity + 3) * group]
-                term = dot(
-                    cells.reshape(rows * width, 3 * group),
-                    weight[k * 3 * group : (k + 1) * 3 * group, :],
-                )
-                total = term if total is None else total + term
-            sides.append(total.reshape(rows, width, chans))
-        return sides
+        products = []
+        for place in range(4):
+            cells = [
+                slab[low + base - 1 + k : high + base - 1 + k, :, place * group : (place + 1) * group]
+                .reshape(rows * width, group)
+                for k in range(3)
+            ]
+            taps = weight[place].reshape(3 * group, chans)
+            products.append(dot(jnp.concatenate(cells, axis=1), taps))
+        first, total, last, spread = products
+        even = (total + spread) + first
+        odd = (total - spread) - last
+        return even.reshape(rows, width, chans), odd.reshape(rows, width, chans)
 
     def keep(row, value):
         return value if row < 2 else jnp.where(valid[row // 2], value, 0.0)
@@ -225,8 +251,8 @@
                 rea_raw[row, :, chans:] = o.astype(BF16)
             put(rea, row + 1, jnp.maximum(e, 0.0), jnp.maximum(o, 0.0))
 
-    def inner_rows(src, weight, bias, dst, low, high):
-        even, odd = conv(src, weight, low, high)
+    def inner_rows(src, weight, bias, dst, low, high, base=1):
+        even, odd = conv(src, weight, low, high, base)
         for row in range(low, high):
             e = jnp.maximum(even[row - low] + bias[...], 0.0)
             o = jnp.maximum(odd[row - low] + bias[...], 0.0)
@@ -248,7 +274,7 @@
                 if row < 2:
                     mer_raw[row, :, lanes] = whole.astype(BF16)
                 outer.append(jnp.maximum(whole, 0.0))
-            put(mer, row + 1, *outer)
+            put(mer, row + 2, *outer)
 
     def carry(row, near, far):
         band = 0.75 * coarse[near].astype(F32) + 0.25 * coarse[far].astype(F32)
@@ -263,36 +289,46 @@
 
     done(lift_in)
     lift(0, 0, (0, 1))
+    send(pj.at[0], pj.at[3], PJ_THREE, me + 3 * step, valid[3])
+    send(coarse.at[0], coarse.at[1], CO_ONE, me + step, valid[1])
+    send(coarse.at[0], coarse.at[2], CO_TWO, me - 2 * step, at_end)
+    done(merge_in)
+    prepare(merge_w)
     received(pj.at[4], PJ_SIB)
     lift(-1, 4, (1,))
-    done(merge_in)
     merge_rows(0, 1)
     send(rea.at[1], rea.at[0], S_REA, sibling)
 
     done(out_in)
     received(coarse.at[3], CO_SIB)
     carry(0, 0, 3)
+    done(fi_in)
+    prepare(fi_w)
+    done(fo_in)
+    prepare(fo_w)
+    pass_on(0)
+    done(si_in)
+    prepare(si_w)
+    done(so_in)
+    prepare(so_w)
+    for k in range(1, PIECES):
+        pass_on(k)
 
     @pl.when(jnp.logical_not(valid[1]))
     def _():
         coarse[1] = coarse[0]
         pj[1] = jnp.zeros_like(pj[1])
 
-    received(pj.at[1], PJ_ONE, valid[1])
-    send(pj.at[1], pj.at[2], PJ_TWO, me + 3 * step, valid[3])
     lift(1, 1, (0, 1))
+    merge_rows(1, 3)
+    received(rea.at[0], S_REA)
+    inner_rows(rea, fi_w, fi_b, in1, 0, 1)
+    send(in1.at[1], in1.at[0], S_IN1, sibling)
     received(coarse.at[1], CO_ONE, valid[1])
     send(coarse.at[1], coarse.at[2], CO_TWO, me + 3 * step, valid[3])
-    merge_rows(1, 3)
-    received(rea.at[0], S_REA)
-    done(fi_in)
-    inner_rows(rea, fi_w, fi_b, in1, 0, 1)
-    send(in1.at[1], in1.at[0], S_IN1, sibling)
     inner_rows(rea, fi_w, fi_b, in1, 1, 2)
-    done(fo_in)
-    received(in1.at[0], S_IN1)
-    merged_rows(0, 1)
-    send(mer.at[1], mer.at[0], S_MER, sibling)
+    carry(1, 0, 1)
+    carry(2, 1, 0)
 
     @pl.when(jnp.logical_not(valid[2]))
     def _():
@@ -302,14 +338,17 @@
     def _():
         pj[3] = jnp.zeros_like(pj[3])
 
-    carry(1, 0, 1)
-    carry(2, 1, 0)
-    received(pj.at[2], PJ_TWO, valid[2])
-    lift(2, 2, (0, 1))
     received(pj.at[3], PJ_THREE, valid[3])
     lift(3, 3, (0,))
+    for k in range(PIECES):
+        received(part(2, k), PJ_TWO + k, valid[2])
+    lift(2, 2, (0, 1))
     merge_rows(3, 6)
     inner_rows(rea, fi_w, fi_b, in1, 2, 5)
+    received(in1.at[0], S_IN1)
+    merged_rows(0, 2)
+    send(mer.at[2], mer.at[1], S_MER, sibling)
+    send(mer.at[3], mer.at[0], S_FAR, sibling)
 
     @pl.when(jnp.logical_not(valid[2]))
     def _():
@@ -317,20 +356,16 @@
 
     received(coarse.at[2], CO_TWO, valid[2])
     carry(3, 1, 2)
-    merged_rows(1, 4)
-    done(si_in)
-    received(mer.at[0], S_MER)
-    inner_rows(mer, si_w, si_b, in2, 0, 1)
-    send(in2.at[1], in2.at[0], S_IN2, sibling)
-    inner_rows(mer, si_w, si_b, in2, 1, 3)
-    done(so_in)
+    merged_rows(2, 4)
+    inner_rows(mer, si_w, si_b, in2, 1, 3, 2)
+    received(mer.at[1], S_MER)
+    received(mer.at[0], S_FAR)
+    inner_rows(mer, si_w, si_b, in2, -1, 1, 2)
 
     line = lax.broadcasted_iota(jnp.int32, (2 * width, 2 * width), 0)
     column = lax.broadcasted_iota(jnp.int32, (2 * width, 2 * width), 1)
     weave = (column == line // 2 + width * (line % 2)).astype(F32).astype(BF16)
     for row in (1, 0):
-        if row == 0:
-            received(in2.at[0], S_IN2)
         sides = conv(in2, so_w, row, row + 1)
         united = [
             (sides[parity][0] + so_b[...] + mer_raw[row, :, parity * chans : (parity + 1) * chans].astype(F32)).astype(BF16)
@@ -353,11 +388,17 @@
     tokens, depth = tap_two.shape
     feat, chans = proj_weight.shape[1], coarse_path.shape[1]
     assert tokens == GW and count % 2 == 0
+    convs = (6, 9, 11, 13, 15)
     args = [arg.reshape(1, -1) if arg.ndim == 1 else arg for arg in args]
+    args = [
+        arg.reshape(3, 3, arg.shape[0] // 9, chans) if place in convs else arg
+        for place, arg in enumerate(args)
+    ]
 
     scratch = []
     for place, arg in enumerate(args):
         shape = (4, *arg.shape) if place == 1 else arg.shape
+        shape = (4, *shape[1:]) if place in convs else shape
         scratch.append(pltpu.VMEM(shape, arg.dtype))
     scratch += [
         pltpu.VMEM((5, tokens, feat), BF16),
@@ -366,12 +407,12 @@
         pltpu.VMEM((4, tokens, 2 * chans), BF16),
         pltpu.VMEM((4, tokens, 2 * chans), F32),
         pltpu.VMEM((6, tokens, 4 * chans), BF16),
-        pltpu.VMEM((5, tokens, 4 * chans), BF16),
+        pltpu.VMEM((6, tokens, 4 * chans), BF16),
         pltpu.VMEM((2, tokens, 2 * chans), BF16),
         pltpu.VMEM((4, tokens, 4 * chans), BF16),
         pltpu.SemaphoreType.DMA((28,)),
-        pltpu.SemaphoreType.DMA((11,)),
-        pltpu.SemaphoreType.DMA((11,)),
+        pltpu.SemaphoreType.DMA((KINDS,)),
+        pltpu.SemaphoreType.DMA((KINDS,)),
     ]
     mid = pl.pallas_call(
         functools.partial(kernel, count),

time: 30.6 us -> 25.8 us (0.84)
  Pallas kernels: 29.4 us -> 24.9 us
    pallas_call x1, Pallas kernels: 29.4 us -> 24.9 us  [body(): pl.pallas_call(functools.partial(kernel, count), out_shape=pltpu.VMEM((2,...]
where the time goes in v2:
time: 25.8 us; the launch traced here: 25.6 us
  Pallas kernels  24.9 us (97%)
  local copies, waits for them, and re-layouts  0.75 us (3%)
    pallas_call x1, Pallas kernels, body(): pl.pallas_call(functools.partial(kernel, count), out_shape=pltpu.VMEM((2,...  24.9 us
    unnamed x1, local copies, waits for them, and re-layouts  0.75 us

profile of v2, /device:TPU:27, one launch (start us, length us, event | category | flops | bytes accessed | tf_op | source)
XLA Modules:
  0.0 25.6 jit_solution(11117148270151348993)
XLA Ops:
  0.0 24.9 %fused_tap.1 = bf16[2,384,256]{2,1,0:T(8,128)(2,1)S(1)} custom-call(bf16[192,1024]{1,0:T(8,128)(2,1)} %tap_h.1, bf16[192,256]{1,0:T(8,128)(2,1)} %coarse_h.1, bf16[1024,512]{1,0:T(8,128)(2,1)} %proj_h.1, f32[1,512]{1,0:T(1,128)} %bitcast.17, bf16[512,2048]{1,0:T(8,128)(2,1)} %lift_h.1, f32[1,512]{1,0:T(1,128)} %bitcast.18, ...), custom_call_target="tpu_custom_call" | custom-call | tf_op jit(solution)/shard_map/fused_tap/pallas_call | solution.py:417
  24.9 0.7 %copy.19 = bf16[2,384,256]{2,1,0:T(8,128)(2,1)} copy(bf16[2,384,256]{2,1,0:T(8,128)(2,1)S(1)} %fused_tap.1) | data formatting | bytes 786432

commit v3 on v2

--- a/solution.py
+++ b/solution.py
@@ -17,6 +17,7 @@
 PJ_TWO = PJ_ONE + PIECES
 KINDS = PJ_TWO + PIECES
 STRIP = 64
+LANES = 128
 
 
 def dot(a, b):
@@ -94,6 +95,7 @@
     mer,
     mer_raw,
     in2,
+    woven,
     local_sem,
     send_sem,
     recv_sem,
@@ -121,10 +123,14 @@
         return [copy]
 
     def fetch_conv(src, dst):
-        copies = []
+        sem = local_sem.at[len(started)]
         for k in range(3):
-            copies += fetch(src.at[side * k + (1 - side) * (2 - k)], dst.at[pl.ds(0, 3), k])
-        return copies
+            pltpu.make_async_copy(
+                src.at[side * k + (1 - side) * (2 - k)], dst.at[pl.ds(0, 3), k], sem
+            ).start()
+        landed = dst.at[pl.ds(0, 3)]
+        started.append(pltpu.make_async_copy(landed, landed, sem))
+        return [started[-1]]
 
     def done(copies):
         for copy in copies:
@@ -134,9 +140,14 @@
     coarse_in = fetch(coarse_h, coarse.at[0])
     lift_in = fetch(lift_bh, lift_b)
     half = 2 * feat
+    lift_sem = local_sem.at[len(started)]
     for m in range(2):
         where = pl.multiple_of((side * m + (1 - side) * (1 - m)) * half, half)
-        lift_in += fetch(lift_h.at[:, pl.ds(where, half)], lift_w.at[:, pl.ds(m * half, half)])
+        pltpu.make_async_copy(
+            lift_h.at[:, pl.ds(where, half)], lift_w.at[:, pl.ds(m * half, half)], lift_sem
+        ).start()
+    started.append(pltpu.make_async_copy(lift_w, lift_w, lift_sem))
+    lift_in.append(started[-1])
 
     partners = (
         (me + step, valid[1]),
@@ -201,16 +212,21 @@
 
     pl.semaphore_wait(barrier, expected)
     at_end = jnp.logical_and(back_two, jnp.logical_not(valid[1]))
+    to_end = jnp.logical_and(
+        jnp.logical_and(back_two, valid[1]), jnp.logical_not(inside(me - 4 * step))
+    )
+    relays = jnp.logical_and(valid[3], inside(me + 5 * step))
     for k in range(PIECES):
         send(part(0, k), part(1, k), PJ_ONE + k, me + step, valid[1])
-        send(part(0, k), part(2, k), PJ_TWO + k, me - 2 * step, at_end)
+    for k in range(PIECES):
+        send(part(0, k), part(2, k), PJ_TWO + k, me - 2 * step, to_end)
     send(pj.at[0], pj.at[4], PJ_SIB, sibling)
     done(coarse_in)
     send(coarse.at[0], coarse.at[3], CO_SIB, sibling)
 
     def pass_on(k):
         received(part(1, k), PJ_ONE + k, valid[1])
-        send(part(1, k), part(2, k), PJ_TWO + k, me + 3 * step, valid[3])
+        send(part(1, k), part(2, k), PJ_TWO + k, me + 3 * step, relays)
 
     def lift(token, slab_token, halves):
         for m in halves:
@@ -277,7 +293,10 @@
             put(mer, row + 2, *outer)
 
     def carry(row, near, far):
-        band = 0.75 * coarse[near].astype(F32) + 0.25 * coarse[far].astype(F32)
+        other = coarse[far].astype(F32)
+        if row == 1:
+            other = jnp.where(valid[1], other, coarse[near].astype(F32))
+        band = 0.75 * coarse[near].astype(F32) + 0.25 * other
         at = lax.broadcasted_iota(jnp.int32, band.shape, 0)
         before = jnp.where(at == 0, band, pltpu.roll(band, 1, 0))
         after = jnp.where(at == width - 1, band, pltpu.roll(band, width - 1, 0))
@@ -287,93 +306,97 @@
                 dot(spread, out_w[...]) + out_b[...]
             )
 
+    def merge_row(row):
+        merge_rows(row, row + 1)
+
+    def first_row(row):
+        inner_rows(rea, fi_w, fi_b, in1, row, row + 1)
+
+    def merged_row(row):
+        merged_rows(row, row + 1)
+
+    def second_row(row):
+        inner_rows(mer, si_w, si_b, in2, row, row + 1, 2)
+
+    def final_row(row):
+        even, odd = conv(in2, so_w, row, row + 1)
+        for parity, value in enumerate((even[0], odd[0])):
+            lanes = slice(parity * chans, (parity + 1) * chans)
+            united = value + so_b[...] + mer_raw[row, :, lanes].astype(F32)
+            for block in range(chans // LANES):
+                cells = united[:, block * LANES : (block + 1) * LANES]
+                woven[row, block, pl.ds(parity, width, stride=2), :] = cells
+        target = side * row + (1 - side) * (1 - row)
+        for block in range(chans // LANES):
+            lanes = slice(block * LANES, (block + 1) * LANES)
+            result[pl.ds(target, 1), :, lanes] = woven[row, block].astype(BF16)[None]
+
     done(lift_in)
     lift(0, 0, (0, 1))
     send(pj.at[0], pj.at[3], PJ_THREE, me + 3 * step, valid[3])
-    send(coarse.at[0], coarse.at[1], CO_ONE, me + step, valid[1])
-    send(coarse.at[0], coarse.at[2], CO_TWO, me - 2 * step, at_end)
     done(merge_in)
     prepare(merge_w)
     received(pj.at[4], PJ_SIB)
     lift(-1, 4, (1,))
-    merge_rows(0, 1)
+    merge_row(0)
     send(rea.at[1], rea.at[0], S_REA, sibling)
-
     done(out_in)
     received(coarse.at[3], CO_SIB)
     carry(0, 0, 3)
     done(fi_in)
     prepare(fi_w)
+    for k in range(PIECES):
+        send(part(0, k), part(2, k), PJ_TWO + k, me - 2 * step, at_end)
+    pass_on(0)
     done(fo_in)
     prepare(fo_w)
-    pass_on(0)
     done(si_in)
     prepare(si_w)
     done(so_in)
     prepare(so_w)
-    for k in range(1, PIECES):
-        pass_on(k)
-
-    @pl.when(jnp.logical_not(valid[1]))
-    def _():
-        coarse[1] = coarse[0]
-        pj[1] = jnp.zeros_like(pj[1])
+    received(rea.at[0], S_REA)
+    pass_on(1)
 
     lift(1, 1, (0, 1))
-    merge_rows(1, 3)
-    received(rea.at[0], S_REA)
-    inner_rows(rea, fi_w, fi_b, in1, 0, 1)
+    merge_row(1)
+    merge_row(2)
+    first_row(0)
+    first_row(1)
     send(in1.at[1], in1.at[0], S_IN1, sibling)
-    received(coarse.at[1], CO_ONE, valid[1])
-    send(coarse.at[1], coarse.at[2], CO_TWO, me + 3 * step, valid[3])
-    inner_rows(rea, fi_w, fi_b, in1, 1, 2)
-    carry(1, 0, 1)
-    carry(2, 1, 0)
-
-    @pl.when(jnp.logical_not(valid[2]))
-    def _():
-        pj[2] = jnp.zeros_like(pj[2])
-
-    @pl.when(jnp.logical_not(valid[3]))
-    def _():
-        pj[3] = jnp.zeros_like(pj[3])
-
+    send(coarse.at[0], coarse.at[1], CO_ONE, me + step, valid[1])
+    send(coarse.at[0], coarse.at[2], CO_TWO, me - 2 * step, back_two)
     received(pj.at[3], PJ_THREE, valid[3])
     lift(3, 3, (0,))
+
     for k in range(PIECES):
         received(part(2, k), PJ_TWO + k, valid[2])
     lift(2, 2, (0, 1))
-    merge_rows(3, 6)
-    inner_rows(rea, fi_w, fi_b, in1, 2, 5)
+    merge_row(3)
+    merge_row(4)
+    first_row(2)
     received(in1.at[0], S_IN1)
-    merged_rows(0, 2)
+    merged_row(0)
+    merge_row(5)
+    first_row(3)
     send(mer.at[2], mer.at[1], S_MER, sibling)
+    first_row(4)
+    received(coarse.at[1], CO_ONE, valid[1])
+    received(coarse.at[2], CO_TWO, valid[2])
+    carry(1, 0, 1)
+    merged_row(1)
+    carry(2, 1, 0)
     send(mer.at[3], mer.at[0], S_FAR, sibling)
-
-    @pl.when(jnp.logical_not(valid[2]))
-    def _():
-        coarse[2] = coarse[1]
-
-    received(coarse.at[2], CO_TWO, valid[2])
+    merged_row(2)
     carry(3, 1, 2)
-    merged_rows(2, 4)
-    inner_rows(mer, si_w, si_b, in2, 1, 3, 2)
+    second_row(1)
+    merged_row(3)
+    second_row(2)
     received(mer.at[1], S_MER)
     received(mer.at[0], S_FAR)
-    inner_rows(mer, si_w, si_b, in2, -1, 1, 2)
-
-    line = lax.broadcasted_iota(jnp.int32, (2 * width, 2 * width), 0)
-    column = lax.broadcasted_iota(jnp.int32, (2 * width, 2 * width), 1)
-    weave = (column == line // 2 + width * (line % 2)).astype(F32).astype(BF16)
-    for row in (1, 0):
-        sides = conv(in2, so_w, row, row + 1)
-        united = [
-            (sides[parity][0] + so_b[...] + mer_raw[row, :, parity * chans : (parity + 1) * chans].astype(F32)).astype(BF16)
-            for parity in range(2)
-        ]
-        woven = dot(weave, jnp.concatenate(united, axis=0)).astype(BF16)
-        target = side * row + (1 - side) * (1 - row)
-        result[pl.ds(target, 1)] = woven[None]
+    second_row(0)
+    second_row(-1)
+    final_row(1)
+    final_row(0)
 
     for copy, there in sent:
         if there is None:
@@ -410,7 +433,8 @@
         pltpu.VMEM((6, tokens, 4 * chans), BF16),
         pltpu.VMEM((2, tokens, 2 * chans), BF16),
         pltpu.VMEM((4, tokens, 4 * chans), BF16),
-        pltpu.SemaphoreType.DMA((28,)),
+        pltpu.VMEM((2, chans // LANES, 2 * tokens, LANES), F32),
+        pltpu.SemaphoreType.DMA((17,)),
         pltpu.SemaphoreType.DMA((KINDS,)),
         pltpu.SemaphoreType.DMA((KINDS,)),
     ]

time: 25.8 us -> 22.8 us (0.88)
  Pallas kernels: 24.9 us -> 21.8 us
    pallas_call x1, Pallas kernels: 24.9 us -> 21.8 us  [body(): pl.pallas_call(functools.partial(kernel, count), out_shape=pltpu.VMEM((2,...]
where the time goes in v3:
time: 22.8 us; the launch traced here: 22.6 us
  Pallas kernels  21.8 us (96%)
  local copies, waits for them, and re-layouts  0.75 us (3%)
    pallas_call x1, Pallas kernels, body(): pl.pallas_call(functools.partial(kernel, count), out_shape=pltpu.VMEM((2,...  21.8 us
    unnamed x1, local copies, waits for them, and re-layouts  0.75 us

profile of v3, /device:TPU:27, one launch (start us, length us, event | category | flops | bytes accessed | tf_op | source)
XLA Modules:
  0.0 22.6 jit_solution(12151984323596503060)
XLA Ops:
  0.0 21.8 %fused_tap.1 = bf16[2,384,256]{2,1,0:T(8,128)(2,1)S(1)} custom-call(bf16[192,1024]{1,0:T(8,128)(2,1)} %tap_h.1, bf16[192,256]{1,0:T(8,128)(2,1)} %coarse_h.1, bf16[1024,512]{1,0:T(8,128)(2,1)} %proj_h.1, f32[1,512]{1,0:T(1,128)} %bitcast.17, bf16[512,2048]{1,0:T(8,128)(2,1)} %lift_h.1, f32[1,512]{1,0:T(1,128)} %bitcast.18, ...), custom_call_target="tpu_custom_call" | custom-call | tf_op jit(solution)/shard_map/fused_tap/pallas_call | solution.py:441
  21.8 0.7 %copy.19 = bf16[2,384,256]{2,1,0:T(8,128)(2,1)} copy(bf16[2,384,256]{2,1,0:T(8,128)(2,1)S(1)} %fused_tap.1) | data formatting | bytes 786432

commit v4 on v3

--- a/solution.py
+++ b/solution.py
@@ -96,6 +96,7 @@
     mer_raw,
     in2,
     woven,
+    early,
     local_sem,
     send_sem,
     recv_sem,
@@ -218,8 +219,6 @@
     relays = jnp.logical_and(valid[3], inside(me + 5 * step))
     for k in range(PIECES):
         send(part(0, k), part(1, k), PJ_ONE + k, me + step, valid[1])
-    for k in range(PIECES):
-        send(part(0, k), part(2, k), PJ_TWO + k, me - 2 * step, to_end)
     send(pj.at[0], pj.at[4], PJ_SIB, sibling)
     done(coarse_in)
     send(coarse.at[0], coarse.at[3], CO_SIB, sibling)
@@ -238,18 +237,29 @@
                 odd = jnp.where(valid[token], odd, 0.0)
             put(wid, 2 * token + m + 1, even, odd)
 
+    def product(slab, weight, row, place, low, high):
+        group = slab.shape[2] // 4
+        lanes = slice(place * group, (place + 1) * group)
+        cells = [slab[row + k, :, lanes] for k in range(low, high)]
+        taps = weight[place, low:high].reshape((high - low) * group, chans)
+        return dot(jnp.concatenate(cells, axis=1), taps)
+
+    early_taps = {1: 2, 2: 1, 3: 2}
+
+    def ahead(row):
+        for place in range(4):
+            early[(row - 1) % 2, place] = product(wid, merge_w, row, place, 0, early_taps[row])
+
     def conv(slab, weight, low, high, base=1):
-        group = slab.shape[2] // 4
         rows = high - low
+        known = early_taps.get(low, 0) if slab is wid else 0
         products = []
         for place in range(4):
-            cells = [
-                slab[low + base - 1 + k : high + base - 1 + k, :, place * group : (place + 1) * group]
-                .reshape(rows * width, group)
-                for k in range(3)
-            ]
-            taps = weight[place].reshape(3 * group, chans)
-            products.append(dot(jnp.concatenate(cells, axis=1), taps))
+            if known:
+                late = product(slab, weight, low, place, known, 3)
+                products.append(late + early[(low - 1) % 2, place])
+            else:
+                products.append(product(slab, weight, low + base - 1, place, 0, 3))
         first, total, last, spread = products
         even = (total + spread) + first
         odd = (total - spread) - last
@@ -338,6 +348,8 @@
     prepare(merge_w)
     received(pj.at[4], PJ_SIB)
     lift(-1, 4, (1,))
+    for k in range(PIECES):
+        send(part(0, k), part(2, k), PJ_TWO + k, me - 2 * step, to_end)
     merge_row(0)
     send(rea.at[1], rea.at[0], S_REA, sibling)
     done(out_in)
@@ -345,8 +357,8 @@
     carry(0, 0, 3)
     done(fi_in)
     prepare(fi_w)
-    for k in range(PIECES):
-        send(part(0, k), part(2, k), PJ_TWO + k, me - 2 * step, at_end)
+    ahead(1)
+    ahead(2)
     pass_on(0)
     done(fo_in)
     prepare(fo_w)
@@ -356,7 +368,8 @@
     prepare(so_w)
     received(rea.at[0], S_REA)
     pass_on(1)
-
+    for k in range(PIECES):
+        send(part(0, k), part(2, k), PJ_TWO + k, me - 2 * step, at_end)
     lift(1, 1, (0, 1))
     merge_row(1)
     merge_row(2)
@@ -367,6 +380,7 @@
     send(coarse.at[0], coarse.at[2], CO_TWO, me - 2 * step, back_two)
     received(pj.at[3], PJ_THREE, valid[3])
     lift(3, 3, (0,))
+    ahead(3)
 
     for k in range(PIECES):
         received(part(2, k), PJ_TWO + k, valid[2])
@@ -434,6 +448,7 @@
         pltpu.VMEM((2, tokens, 2 * chans), BF16),
         pltpu.VMEM((4, tokens, 4 * chans), BF16),
         pltpu.VMEM((2, chans // LANES, 2 * tokens, LANES), F32),
+        pltpu.VMEM((2, 4, tokens, chans), F32),
         pltpu.SemaphoreType.DMA((17,)),
         pltpu.SemaphoreType.DMA((KINDS,)),
         pltpu.SemaphoreType.DMA((KINDS,)),

time: 22.8 us -> 21.5 us (0.943)
  Pallas kernels: 21.8 us -> 20.3 us
    pallas_call x1, Pallas kernels: 21.8 us -> 20.3 us  [body(): pl.pallas_call(functools.partial(kernel, count), out_shape=pltpu.VMEM((2,...]
where the time goes in v4:
time: 21.5 us; the launch traced here: 21.1 us
  Pallas kernels  20.3 us (94%)
  local copies, waits for them, and re-layouts  0.75 us (3%)
    pallas_call x1, Pallas kernels, body(): pl.pallas_call(functools.partial(kernel, count), out_shape=pltpu.VMEM((2,...  20.3 us
    unnamed x1, local copies, waits for them, and re-layouts  0.75 us

profile of v4, /device:TPU:27, one launch (start us, length us, event | category | flops | bytes accessed | tf_op | source)
XLA Modules:
  0.0 21.1 jit_solution(12917904190298558006)
XLA Ops:
  0.0 20.3 %fused_tap.1 = bf16[2,384,256]{2,1,0:T(8,128)(2,1)S(1)} custom-call(bf16[192,1024]{1,0:T(8,128)(2,1)} %tap_h.1, bf16[192,256]{1,0:T(8,128)(2,1)} %coarse_h.1, bf16[1024,512]{1,0:T(8,128)(2,1)} %proj_h.1, f32[1,512]{1,0:T(1,128)} %bitcast.17, bf16[512,2048]{1,0:T(8,128)(2,1)} %lift_h.1, f32[1,512]{1,0:T(1,128)} %bitcast.18, ...), custom_call_target="tpu_custom_call" | custom-call | tf_op jit(solution)/shard_map/fused_tap/pallas_call | solution.py:456
  20.3 0.7 %copy.19 = bf16[2,384,256]{2,1,0:T(8,128)(2,1)} copy(bf16[2,384,256]{2,1,0:T(8,128)(2,1)S(1)} %fused_tap.1) | data formatting | bytes 786432

commit v5 on v4

--- a/solution.py
+++ b/solution.py
@@ -392,8 +392,8 @@
     merged_row(0)
     merge_row(5)
     first_row(3)
+    first_row(4)
     send(mer.at[2], mer.at[1], S_MER, sibling)
-    first_row(4)
     received(coarse.at[1], CO_ONE, valid[1])
     received(coarse.at[2], CO_TWO, valid[2])
     carry(1, 0, 1)

time: 21.5 us -> 21.3 us (level)
  no operation moved by 1% of the time
where the time goes in v5:
time: 21.3 us; the launch traced here: 21 us
  Pallas kernels  20.3 us (95%)
  local copies, waits for them, and re-layouts  0.75 us (4%)
    pallas_call x1, Pallas kernels, body(): pl.pallas_call(functools.partial(kernel, count), out_shape=pltpu.VMEM((2,...  20.3 us
    unnamed x1, local copies, waits for them, and re-layouts  0.75 us

profile of v5, /device:TPU:27, one launch (start us, length us, event | category | flops | bytes accessed | tf_op | source)
XLA Modules:
  0.0 21.0 jit_solution(10336850482022220770)
XLA Ops:
  0.0 20.3 %fused_tap.1 = bf16[2,384,256]{2,1,0:T(8,128)(2,1)S(1)} custom-call(bf16[192,1024]{1,0:T(8,128)(2,1)} %tap_h.1, bf16[192,256]{1,0:T(8,128)(2,1)} %coarse_h.1, bf16[1024,512]{1,0:T(8,128)(2,1)} %proj_h.1, f32[1,512]{1,0:T(1,128)} %bitcast.17, bf16[512,2048]{1,0:T(8,128)(2,1)} %lift_h.1, f32[1,512]{1,0:T(1,128)} %bitcast.18, ...), custom_call_target="tpu_custom_call" | custom-call | tf_op jit(solution)/shard_map/fused_tap/pallas_call | solution.py:456
  20.3 0.7 %copy.19 = bf16[2,384,256]{2,1,0:T(8,128)(2,1)} copy(bf16[2,384,256]{2,1,0:T(8,128)(2,1)S(1)} %fused_tap.1) | data formatting | bytes 786432
